TPU v7x, 32 devices: a whole 2x2x4 slice. The times are simulated.
32 devices in a mesh: replica: 8 (over z, y), shard: 4 (over x, core).
Axes of the slice: x: 2, y: 2, z: 4, core: 2. Of those that a mesh axis runs over, the one named last changes fastest.
Arguments:
- outer_params: float32 [512, 4096], P('shard'), may hold values from -6 to 6, as said below
- local_params: bfloat16 [8, 512, 4096], P('replica', 'shard'), may hold values from -70 to 70
- momentum: float32 [512, 4096], P('shard'), may hold values from -6 to 6
Outputs:
- params_next: float32 [512, 4096], P('shard')
- momentum_next: float32 [512, 4096], P('shard')
- block_scales: float32 [32, 512], P(None, 'shard')
Inputs may be any that keep to these rules, and one draw needn't show every extreme that they name: `outer_params`: outer parameters of order one.
All inputs are finite; a program needn't handle non-finite values.
Results may differ from a plain program's by a relative error of at most 0.005.
Values may be sent and summed in bfloat16 or wider, within the bound.
A program may use at most 64 MiB of HBM per device.

v0:
```python
import math

import jax
import jax.numpy as jnp
from jax import lax
from jax.sharding import PartitionSpec as P

BLOCK = 128


epsilon = 1e-06
clip_level = 0.5
outer_rate = 0.7
outer_decay = 0.9
grid_levels = 7.0


def smooth_step(values):
    return values - jnp.sin(2.0 * math.pi * values) / (2.0 * math.pi)


def smooth_round(values):
    return smooth_step(smooth_step(values))


def block_max(values):
    return jnp.max(
        jnp.abs(values).reshape(values.shape[0], values.shape[1] // BLOCK, BLOCK), axis=2
    )


def per_device(outer_params, local_params, momentum):
    workers = lax.axis_size("replica")
    row_count = outer_params.shape[0]
    col_count = outer_params.shape[1]
    slice_rows = row_count // workers
    slice_start = lax.axis_index("replica") * slice_rows
    deltas = outer_params - local_params[0].astype(jnp.float32)
    absmax = lax.pmax(block_max(deltas), "replica")
    spread_scale = jnp.repeat(absmax + epsilon, BLOCK, axis=1)
    encoded = smooth_round(grid_levels * deltas / spread_scale).astype(jnp.bfloat16)
    arrived = lax.all_to_all(encoded[None], "replica", split_axis=1, concat_axis=0, tiled=True)
    slice_scale = lax.dynamic_slice_in_dim(spread_scale, slice_start, slice_rows, 0)
    summed_rows = jnp.sum(arrived.astype(jnp.float32), axis=0) * slice_scale / grid_levels
    gradient_slice = summed_rows / workers
    square_total = lax.psum(jnp.sum(gradient_slice * gradient_slice), ("replica", "shard"))
    entry_count = row_count * lax.axis_size("shard") * col_count
    root_mean = jnp.sqrt(square_total / entry_count + epsilon)
    factor = jnp.minimum(1.0, clip_level / root_mean)
    gradient = lax.all_gather(gradient_slice, "replica", axis=0, tiled=True)
    clipped = factor * gradient
    momentum_next = outer_decay * momentum + clipped
    params_next = outer_params - outer_rate * (clipped + outer_decay * momentum_next)
    return (params_next, momentum_next, absmax.T)


def solution(mesh):
    return jax.shard_map(
        per_device,
        mesh=mesh,
        in_specs=(P("shard", None), P("replica", "shard", None), P("shard", None)),
        out_specs=(P("shard", None), P("shard", None), P(None, "shard")),
        check_vma=False,
    )
```

profile of v0, /device:TPU:0, one launch (start us, length us, event | category | flops | bytes accessed | tf_op | source)
XLA Modules:
  0.0 172.0 jit_solution(18044409390670645208)
XLA Ops:
  7.2 2.1 %abs_bitcast_fusion = f32[16,8,32,128]{3,1,2,0:T(8,128)S(1)} fusion(f32[128,4096]{1,0:T(8,128)} %param.3, bf16[1,128,4096]{2,1,0:T(8,128)(2,1)} %param.4), kind=kLoop, calls=%fused_computation.5 | loop fusion | flops 1572864 | bytes 5242880
  9.3 0.4 copy.11
  9.7 0.0 copy-start.1
  9.7 0.6 reduce_max.9
  10.3 39.3 %pmax.7 = f32[128,32]{1,0:T(8,128)S(1)} all-reduce(f32[128,32]{1,0:T(8,128)S(1)} %reduce_max.9), channel_id=1, replica_groups=mesh['replica'=8,'shard'=4] {'replica'}, use_global_device_ids=true, to_apply=%region_1.0 | all-reduce | flops 4096 | bytes 32768 | tf_op jit(solution)/shard_map/pmax | solution.py:39
  49.6 0.6 broadcast_in_dim.6
  50.2 0.0 copy-done.1
  50.2 15.9 %fusion = bf16[1,128,4096]{2,1,0:T(8,128)(2,1)S(1)} fusion(f32[128,4096]{1,0:T(8,128)} %param.3, bf16[1,128,4096]{2,1,0:T(8,128)(2,1)S(1)} %copy-done.1, f32[16,8,32,128]{3,2,1,0:T(8,128)S(1)} %bitcast.23), kind=kLoop, calls=%fused_computation.6 | loop fusion | flops 5767168 | bytes 6291456 | tf_op jit(solution)/shard_map/broadcast_in_dim | solution.py:42
  66.1 3.7 %copy.18 = bf16[1,128,4096]{2,0,1:T(2,128)(2,1)} copy(bf16[1,128,4096]{2,1,0:T(8,128)(2,1)S(1)} %fusion) | data formatting | bytes 2097152 | tf_op jit(solution)/shard_map/broadcast_in_dim | solution.py:42
  69.8 0.5 broadcast.25
  70.3 8.4 %reduce = bf16[128,4096]{1,0:T(8,128)(2,1)S(1)} reduce(bf16[128,1,4096]{2,1,0:T(2,128)(2,1)} %bitcast.26, bf16[]{:T(256)} %broadcast.25), dimensions={1}, to_apply=%bitcast.22.reduce_sub_computation | reduce | bytes 2097154
  78.7 1.6 reshape.23
  80.3 3.6 %all-to-all-start = ((bf16[8,2,32768]{2,1,0:T(2,128)(2,1)}), bf16[8,2,32768]{2,1,0:T(2,128)(2,1)S(1)}, u32[]{:S(2)}, u32[]{:S(2)}) async-start(bf16[8,2,32768]{2,1,0:T(2,128)(2,1)} %reshape.23), calls=%async_computation | async-start | bytes 2097152 | tf_op jit(solution)/shard_map/all_to_all | solution.py:42
  83.8 0.2 all-gather.2.cloned.1.call-start
  84.1 3.0 %copy.17 = f32[16,8,32,128]{3,1,2,0:T(8,128)} copy(f32[16,8,32,128]{3,2,1,0:T(8,128)S(1)} %bitcast.24) | data formatting | bytes 4194304
  87.0 15.8 %all-to-all-done = bf16[8,2,32768]{2,1,0:T(2,128)(2,1)S(1)} async-done(((bf16[8,2,32768]{2,1,0:T(2,128)(2,1)}), bf16[8,2,32768]{2,1,0:T(2,128)(2,1)S(1)}, u32[]{:S(2)}, u32[]{:S(2)}) %all-to-all-start) | async-done | bytes 1048608 | tf_op jit(solution)/shard_map/all_to_all | solution.py:42
  102.8 1.0 reshape.24
  103.8 3.0 %copy.10 = f32[1,128,4096]{2,1,0:T(8,128)} copy(bf16[1,128,4096]{2,0,1:T(2,128)(2,1)S(1)} %bitcast.28) | data formatting | bytes 3145728
  106.8 0.0 copy-start
  106.8 1.9 %reduce_sum.18 = f32[16,4096]{1,0:T(8,128)S(1)} reduce(f32[8,16,4096]{2,1,0:T(8,128)} %bitcast.25, f32[]{:T(128)} %constant.13.clone.1), dimensions={0}, to_apply=%region_2.0 | reduce | flops 458752 | bytes 2359300 | tf_op jit(solution)/shard_map/reduce_sum | solution.py:44
  108.7 2.3 %multiply_reduce_fusion = (f32[]{:T(128)}, f32[16,4096]{1,0:T(8,128)}) fusion(f32[16,4096]{1,0:T(8,128)S(1)} %reduce_sum.18, f32[128,4096]{1,0:T(8,128)} %bitcast.29, s32[]{:T(128)S(6)} %select_n.3), kind=kLoop, calls=%fused_computation.7 | loop fusion | flops 262143 | bytes 786440 | tf_op jit(solution)/shard_map/reduce_sum | solution.py:46
  111.0 0.0 all-gather.2.cloned.1.call-update
  111.0 0.7 copy.9
  111.7 39.4 %psum.7 = f32[]{:T(128)} all-reduce(f32[]{:T(128)} %get-tuple-element.11), channel_id=1, replica_groups=mesh['replica'=8,'shard'=4] {'replica','shard'}, use_global_device_ids=true, to_apply=%region_4.0 | all-reduce | flops 1 | bytes 8 | tf_op jit(solution)/shard_map/psum | solution.py:46
  151.7 8.5 %all-gather.2.cloned.1.call-done = f32[128,4096]{1,0:T(8,128)} async-done(((f32[16,4096]{1,0:T(8,128)}), f32[128,4096]{1,0:T(8,128)}) %all-gather.2.cloned.1.call-update) | async-done | bytes 2097168 | tf_op jit(solution)/shard_map/all_gather | solution.py:50
  160.2 0.0 copy-done
  160.2 4.9 %multiply_subtract_fusion = (f32[128,4096]{1,0:T(8,128)}, f32[128,4096]{1,0:T(8,128)}) fusion(f32[128,4096]{1,0:T(8,128)S(1)} %copy-done, f32[128,4096]{1,0:T(8,128)} %all-gather.2.cloned.1.call-done, f32[]{:T(128)S(6)} %min_shard_map.3, f32[128,4096]{1,0:T(8,128)} %param.5), kind=kLoop, calls=%fused_computation.2 | loop fusion | flops 3670016 | bytes 10485764 | tf_op jit(solution)/shard_map/sub | solution.py:53
  (1 shorter events, 0.0 us)
Async XLA Ops:
  9.7 40.6 %copy-start.1 = (bf16[1,128,4096]{2,1,0:T(8,128)(2,1)S(1)}, bf16[1,128,4096]{2,1,0:T(8,128)(2,1)}, u32[]{:S(2)}) copy-start(bf16[1,128,4096]{2,1,0:T(8,128)(2,1)} %param.4) | copy-start | bytes 3145732
  80.3 22.5 %all-to-all-start = ((bf16[8,2,32768]{2,1,0:T(2,128)(2,1)}), bf16[8,2,32768]{2,1,0:T(2,128)(2,1)S(1)}, u32[]{:S(2)}, u32[]{:S(2)}) async-start(bf16[8,2,32768]{2,1,0:T(2,128)(2,1)} %reshape.23), calls=%async_computation | async-start | bytes 2097152 | tf_op jit(solution)/shard_map/all_to_all | solution.py:42
  83.8 76.4 %all-gather.2.cloned.1.call-start = ((), (), s32[]{:S(2)}) async-start(), calls=%async_computation.1 | async-start | bytes 2359296 | tf_op jit(solution)/shard_map/all_gather | solution.py:50
  106.8 53.4 %copy-start = (f32[128,4096]{1,0:T(8,128)S(1)}, f32[128,4096]{1,0:T(8,128)}, u32[]{:S(2)}) copy-start(f32[128,4096]{1,0:T(8,128)} %param.3) | copy-start | bytes 6291460
Sparse Core Ops, SparseCore 0:
  111.1 49.0 all-gather.1
where the time goes:
time: 172 us
  blocking collectives  78.7 us (46%)
  other arithmetic  36 us (21%)
  waiting for transfers between devices  24.3 us (14%)
  between operations  14.8 us (9%)
  local copies, waits for them, and re-layouts  14.4 us (8%)
  starting transfers between devices  3.78 us (2%)
    psum x1, blocking collectives, per_device(): lax.psum(jnp.sum(gradient_slice * gradient_slice), ('replica', 'shard'))  39.4 us
    pmax x1, blocking collectives, per_device(): absmax = lax.pmax(block_max(deltas), 'replica')  39.3 us
    broadcast_in_dim x1, other arithmetic, per_device(): encoded[None]  15.9 us
    all_to_all x1, waiting for transfers between devices, per_device(): lax.all_to_all(encoded[None], 'replica', split_axis=1, concat_axis=0, til...  15.8 us
    unnamed x2, other arithmetic  10.5 us
    unnamed x11, local copies, waits for them, and re-layouts  10.1 us
    all_gather x1, waiting for transfers between devices, per_device(): gradient = lax.all_gather(gradient_slice, 'replica', axis=0, tiled=True)  8.49 us
    sub x1, other arithmetic, per_device(): outer_params - outer_rate * (clipped + outer_decay * momentum_next)  4.9 us
  transfers between devices with their start and end apart: 2, of which 2 were waited for; matrix products, arithmetic and copies ran while one was open for 2% of the time, Pallas kernels for 0%

commit v1 on v0

v1 whole, which is shorter than its diff:
```python
import functools

import jax
import jax.numpy as jnp
from jax import lax
from jax.experimental import pallas as pl
from jax.experimental.pallas import tpu as pltpu
from jax.sharding import PartitionSpec as P

BLOCK = 128
MESH = pl.DeviceIdType.MESH

epsilon = 1e-06
clip_level = 0.5
outer_rate = 0.7
outer_decay = 0.9
grid_levels = 7.0

SMOOTH = (6.57973588, -12.98785441, 12.20756634, -6.687892761, 2.368806331, -0.5120006377)
SHIFT = 1.5 * 2.0**23


def smooth_rest(rest):
    square = rest * rest
    value = SMOOTH[-1]
    for coefficient in SMOOTH[-2::-1]:
        value = value * square + coefficient
    return rest * square * value


def column_of(row):
    return jnp.broadcast_to(row, (BLOCK, row.shape[1])).T


def exchange_kernel(
    workers, shards, entry_count,
    outer_hbm, local_hbm, grad_out, max_out, factor_out,
    outer_v, local_v, max_slots, inverse, spread, encoded, arrived, total, share, squares, shard_squares,
    load_sem, max_send, max_recv, enc_send, enc_recv, sq_send, sq_recv, ss_send, ss_recv, gat_send, gat_recv, own_sem,
):
    me = lax.axis_index("replica")
    my_shard = lax.axis_index("shard")
    rows, cols = outer_v.shape
    blocks = cols // BLOCK
    width = cols // workers
    blocks_each = width // BLOCK
    pieces = load_sem.shape[1]
    piece = cols // pieces

    def peer(step):
        return lax.rem(me + step, workers)

    def origin(step):
        return lax.rem(me + workers - step, workers)

    def loads(i):
        part = pl.ds(i * piece, piece)
        return (
            pltpu.make_async_copy(outer_hbm.at[:, part], outer_v.at[:, part], load_sem.at[0, i]),
            pltpu.make_async_copy(local_hbm.at[0, :, part], local_v.at[:, part], load_sem.at[1, i]),
        )

    for i in range(pieces):
        for copy in loads(i):
            copy.start()

    barrier = pltpu.get_barrier_semaphore()

    @pl.loop(1, workers)
    def _(step):
        pl.semaphore_signal(barrier, inc=1, device_id={"replica": peer(step)}, device_id_type=MESH)

    @pl.loop(1, shards)
    def _(step):
        pl.semaphore_signal(
            barrier, inc=1, device_id={"shard": lax.rem(my_shard + step, shards)}, device_id_type=MESH
        )

    def delta(block):
        at = pl.ds(pl.multiple_of(block * BLOCK, BLOCK), BLOCK)
        return outer_v[:, at] - local_v[:, at].astype(jnp.float32)

    per_piece = piece // BLOCK
    for i in range(pieces):
        for copy in loads(i):
            copy.wait()

        @pl.loop(i * per_piece, (i + 1) * per_piece)
        def _(block):
            max_slots[me, pl.ds(block, 1), :] = jnp.max(jnp.abs(delta(block)).T, axis=0, keepdims=True)

    pl.semaphore_wait(barrier, workers + shards - 2)

    def max_copy(step):
        return pltpu.make_async_remote_copy(
            src_ref=max_slots.at[me], dst_ref=max_slots.at[me],
            send_sem=max_send.at[step], recv_sem=max_recv.at[step],
            device_id={"replica": peer(step)}, device_id_type=MESH,
        )

    @pl.loop(1, workers)
    def _(step):
        max_copy(step).start()

    @pl.loop(1, workers)
    def _(step):
        max_copy(step).wait()

    absmax = max_slots[0]
    for w in range(1, workers):
        absmax = jnp.maximum(absmax, max_slots[w])
    max_out[...] = absmax
    inverse[...] = grid_levels / (absmax + epsilon)
    spread[...] = (absmax + epsilon) / (grid_levels * workers)

    def encode(target, put):
        for i in range(blocks_each):
            block = target * blocks_each + i
            values = delta(block) * column_of(inverse[pl.ds(block, 1), :])
            nearest = (values + SHIFT) - SHIFT
            rest = smooth_rest(smooth_rest(values - nearest))
            put(i, (nearest + rest).astype(jnp.bfloat16))

    def enc_copy(step):
        return pltpu.make_async_remote_copy(
            src_ref=encoded.at[peer(step)], dst_ref=arrived.at[me],
            send_sem=enc_send.at[step], recv_sem=enc_recv.at[step],
            device_id={"replica": peer(step)}, device_id_type=MESH,
        )

    @pl.loop(1, workers)
    def _(step):
        target = peer(step)

        def put(i, value):
            encoded[target, :, i * BLOCK : (i + 1) * BLOCK] = value

        encode(target, put)

        @pl.when(step > 1)
        def _():
            enc_copy(step - 1).start()

    def put_own(i, value):
        total[:, i * BLOCK : (i + 1) * BLOCK] = value.astype(jnp.float32)

    encode(me, put_own)
    enc_copy(workers - 1).start()

    @pl.loop(1, workers)
    def _(step):
        enc_copy(step).wait()
        total[...] += arrived[origin(step)].astype(jnp.float32)

    square = jnp.zeros((8, BLOCK), jnp.float32)
    for i in range(blocks_each):
        block = me * blocks_each + i
        value = total[:, i * BLOCK : (i + 1) * BLOCK] * column_of(spread[pl.ds(block, 1), :])
        share[:, i * BLOCK : (i + 1) * BLOCK] = value.astype(jnp.bfloat16)
        square = square + jnp.sum((value * value).reshape(rows // 8, 8, BLOCK), axis=0)
    squares[me] = jnp.broadcast_to(jnp.sum(square, axis=0, keepdims=True), (8, BLOCK))

    def sq_copy(step):
        return pltpu.make_async_remote_copy(
            src_ref=squares.at[me], dst_ref=squares.at[me],
            send_sem=sq_send.at[step], recv_sem=sq_recv.at[step],
            device_id={"replica": peer(step)}, device_id_type=MESH,
        )

    def place(worker):
        return grad_out.at[:, pl.ds(pl.multiple_of(worker * width, BLOCK), width)]

    def gat_copy(step):
        return pltpu.make_async_remote_copy(
            src_ref=share, dst_ref=place(me),
            send_sem=gat_send.at[step], recv_sem=gat_recv.at[step],
            device_id={"replica": peer(step)}, device_id_type=MESH,
        )

    @pl.loop(1, workers)
    def _(step):
        sq_copy(step).start()

    @pl.loop(1, workers)
    def _(step):
        gat_copy(step).start()

    own = pltpu.make_async_copy(share, place(me), own_sem)
    own.start()

    @pl.loop(1, workers)
    def _(step):
        sq_copy(step).wait()

    part = squares[0]
    for w in range(1, workers):
        part = part + squares[w]
    shard_squares[my_shard] = part

    def ss_copy(step):
        return pltpu.make_async_remote_copy(
            src_ref=shard_squares.at[my_shard], dst_ref=shard_squares.at[my_shard],
            send_sem=ss_send.at[step], recv_sem=ss_recv.at[step],
            device_id={"shard": lax.rem(my_shard + step, shards)}, device_id_type=MESH,
        )

    @pl.loop(1, shards)
    def _(step):
        ss_copy(step).start()

    @pl.loop(1, shards)
    def _(step):
        ss_copy(step).wait()

    part = shard_squares[0]
    for s in range(1, shards):
        part = part + shard_squares[s]
    mean = jnp.sum(part, axis=1, keepdims=True) / entry_count
    root_mean = jnp.sqrt(mean + epsilon)
    factor_out[...] = jnp.broadcast_to(jnp.minimum(1.0, clip_level / root_mean), factor_out.shape)

    own.wait()

    @pl.loop(1, workers)
    def _(step):
        gat_copy(step).wait()


def exchange(outer_params, local_params):
    workers = lax.axis_size("replica")
    shards = lax.axis_size("shard")
    rows, cols = outer_params.shape
    blocks = cols // BLOCK
    width = cols // workers
    dma = pltpu.SemaphoreType.DMA
    vmem = pl.BlockSpec(memory_space=pltpu.VMEM)
    anywhere = pl.BlockSpec(memory_space=pl.ANY)
    return pl.pallas_call(
        functools.partial(exchange_kernel, workers, shards, rows * shards * cols),
        out_shape=(
            jax.ShapeDtypeStruct((rows, cols), jnp.bfloat16),
            jax.ShapeDtypeStruct((blocks, rows), jnp.float32),
            jax.ShapeDtypeStruct((8, BLOCK), jnp.float32),
        ),
        in_specs=[anywhere, anywhere],
        out_specs=(anywhere, vmem, vmem),
        scratch_shapes=[
            pltpu.VMEM((rows, cols), jnp.float32),
            pltpu.VMEM((rows, cols), jnp.bfloat16),
            pltpu.VMEM((workers, blocks, rows), jnp.float32),
            pltpu.VMEM((blocks, rows), jnp.float32),
            pltpu.VMEM((blocks, rows), jnp.float32),
            pltpu.VMEM((workers, rows, width), jnp.bfloat16),
            pltpu.VMEM((workers, rows, width), jnp.bfloat16),
            pltpu.VMEM((rows, width), jnp.float32),
            pltpu.VMEM((rows, width), jnp.bfloat16),
            pltpu.VMEM((workers, 8, BLOCK), jnp.float32),
            pltpu.VMEM((shards, 8, BLOCK), jnp.float32),
            dma((2, 4)),
            dma((workers,)), dma((workers,)),
            dma((workers,)), dma((workers,)),
            dma((workers,)), dma((workers,)),
            dma((shards,)), dma((shards,)),
            dma((workers,)), dma((workers,)),
            dma(()),
        ],
        compiler_params=pltpu.CompilerParams(
            collective_id=0, has_side_effects=True, vmem_limit_bytes=16 * 2**20
        ),
        cost_estimate=pl.CostEstimate(
            flops=50 * rows * cols, bytes_accessed=8 * rows * cols * 4, transcendentals=0
        ),
    )(outer_params, local_params)


def per_device(outer_params, local_params, momentum):
    gradient, absmax, factor = exchange(outer_params, local_params)
    clipped = factor[0, 0] * gradient.astype(jnp.float32)
    momentum_next = outer_decay * momentum + clipped
    params_next = outer_params - outer_rate * (clipped + outer_decay * momentum_next)
    return (params_next, momentum_next, absmax)


def solution(mesh):
    return jax.shard_map(
        per_device,
        mesh=mesh,
        in_specs=(P("shard", None), P("replica", "shard", None), P("shard", None)),
        out_specs=(P("shard", None), P("shard", None), P(None, "shard")),
        check_vma=False,
    )
```

time: 172 us -> 72 us (0.42)
  the two profiles are of different devices: /device:TPU:0 before, /device:TPU:29 now
where the time goes in v1:
time: 72 us; the launch traced here: 71.8 us
  Pallas kernels  62.2 us (86%)
  other arithmetic  5.01 us (7%)
  local copies, waits for them, and re-layouts  3.93 us (5%)
    pallas_call x1, Pallas kernels, exchange(): pl.pallas_call(functools.partial(exchange_kernel, workers, shards, rows *...  62.2 us
    sub x1, other arithmetic, per_device(): outer_params - outer_rate * (clipped + outer_decay * momentum_next)  5.01 us
    unnamed x7, local copies, waits for them, and re-layouts  3.42 us

profile of v1, /device:TPU:29, one launch (start us, length us, event | category | flops | bytes accessed | tf_op | source)
XLA Modules:
  0.0 71.8 jit_solution(18043747182808896472)
XLA Ops:
  0.6 0.0 copy-start
  0.6 1.6 %copy-done = f32[128,4096]{1,0:T(8,128)S(1)} copy-done((f32[128,4096]{1,0:T(8,128)S(1)}, f32[128,4096]{1,0:T(8,128)}, u32[]{:S(2)}) %copy-start) | copy-done | bytes 2097176
  2.2 0.0 copy-start.2
  2.2 1.2 %copy-done.2 = bf16[1,128,4096]{2,1,0:T(8,128)(2,1)S(1)} copy-done((bf16[1,128,4096]{2,1,0:T(8,128)(2,1)S(1)}, bf16[1,128,4096]{2,1,0:T(8,128)(2,1)}, u32[]{:S(2)}) %copy-start.2) | copy-done | bytes 1048600
  3.4 0.0 copy-start.1
  3.4 62.2 %shard_map.58 = (bf16[128,4096]{1,0:T(8,128)(2,1)S(1)}, f32[32,128]{1,0:T(8,128)S(1)}, f32[8,128]{1,0:T(8,128)S(1)}) custom-call(f32[128,4096]{1,0:T(8,128)S(1)} %copy-done, bf16[1,128,4096]{2,1,0:T(8,128)(2,1)S(1)} %copy-done.2), custom_call_target="tpu_custom_call" | custom-call | flops 26214400 | bytes 16777216 | tf_op jit(solution)/shard_map/pallas_call | solution.py:238
  65.6 0.5 slice.3
  66.1 0.0 copy-done.1
  66.2 5.0 %multiply_subtract_fusion = (f32[128,4096]{1,0:T(8,128)}, f32[128,4096]{1,0:T(8,128)}) fusion(f32[128,4096]{1,0:T(8,128)S(1)} %copy-done.1, bf16[128,4096]{1,0:T(8,128)(2,1)S(1)} %get-tuple-element.7, f32[]{:T(128)} %bitcast, f32[128,4096]{1,0:T(8,128)} %param.5), kind=kLoop, calls=%fused_computation | loop fusion | flops 4194304 | bytes 9437188 | tf_op jit(solution)/shard_map/sub | solution.py:280
  71.2 0.6 copy.7
Async XLA Ops:
  0.6 1.6 %copy-start = (f32[128,4096]{1,0:T(8,128)S(1)}, f32[128,4096]{1,0:T(8,128)}, u32[]{:S(2)}) copy-start(f32[128,4096]{1,0:T(8,128)} %outer_hbm.1) | copy-start | bytes 6291460
  2.2 1.2 %copy-start.2 = (bf16[1,128,4096]{2,1,0:T(8,128)(2,1)S(1)}, bf16[1,128,4096]{2,1,0:T(8,128)(2,1)}, u32[]{:S(2)}) copy-start(bf16[1,128,4096]{2,1,0:T(8,128)(2,1)} %local_hbm.1) | copy-start | bytes 3145732
  3.4 62.7 %copy-start.1 = (f32[128,4096]{1,0:T(8,128)S(1)}, f32[128,4096]{1,0:T(8,128)}, u32[]{:S(2)}) copy-start(f32[128,4096]{1,0:T(8,128)} %outer_hbm.1) | copy-start | bytes 6291460

commit v2 on v1

v2 whole, which is shorter than its diff:
```python
import functools

import jax
import jax.numpy as jnp
from jax import lax
from jax.experimental import pallas as pl
from jax.experimental.pallas import tpu as pltpu
from jax.sharding import PartitionSpec as P

BLOCK = 128
MESH = pl.DeviceIdType.MESH

epsilon = 1e-06
clip_level = 0.5
outer_rate = 0.7
outer_decay = 0.9
grid_levels = 7.0

SMOOTH = (6.57973588, -12.98785441, 12.20756634, -6.687892761, 2.368806331, -0.5120006377)
SHIFT = 1.5 * 2.0**23


def smooth_rest(rest):
    square = rest * rest
    value = SMOOTH[-1]
    for coefficient in SMOOTH[-2::-1]:
        value = value * square + coefficient
    return rest * square * value


def column_of(row):
    return jnp.broadcast_to(row, (BLOCK, row.shape[1])).T


def exchange_kernel(
    workers, shards, entry_count,
    outer_hbm, local_hbm, momentum_hbm, grad_out, momentum_out, max_out, factor_out,
    outer_v, local_v, max_slots, inverse, spread, encoded, arrived, total, share, squares, shard_squares,
    load_sem, max_send, max_recv, enc_send, enc_recv, sq_send, sq_recv, ss_send, ss_recv, gat_send, gat_recv, fwd_send, fwd_recv, own_sem, momentum_sem,
):
    me = lax.axis_index("replica")
    my_shard = lax.axis_index("shard")
    rows, cols = outer_v.shape
    blocks = cols // BLOCK
    width = cols // workers
    blocks_each = width // BLOCK
    parts, half = share.shape[:2]
    pieces = load_sem.shape[1]
    piece = cols // pieces

    def peer(step):
        return lax.rem(me + step, workers)

    def origin(step):
        return lax.rem(me + workers - step, workers)

    def loads(i):
        part = pl.ds(i * piece, piece)
        return (
            pltpu.make_async_copy(outer_hbm.at[:, part], outer_v.at[:, part], load_sem.at[0, i]),
            pltpu.make_async_copy(local_hbm.at[0, :, part], local_v.at[:, part], load_sem.at[1, i]),
        )

    for i in range(pieces):
        for copy in loads(i):
            copy.start()
    momentum_copy = pltpu.make_async_copy(momentum_hbm, momentum_out, momentum_sem)

    barrier = pltpu.get_barrier_semaphore()

    @pl.loop(1, workers)
    def _(step):
        pl.semaphore_signal(barrier, inc=1, device_id={"replica": peer(step)}, device_id_type=MESH)

    @pl.loop(1, shards)
    def _(step):
        pl.semaphore_signal(
            barrier, inc=1, device_id={"shard": lax.rem(my_shard + step, shards)}, device_id_type=MESH
        )

    def delta(block, rows_at=slice(None)):
        at = pl.ds(pl.multiple_of(block * BLOCK, BLOCK), BLOCK)
        return outer_v[rows_at, at] - local_v[rows_at, at].astype(jnp.float32)

    per_piece = piece // BLOCK
    for i in range(pieces):
        for copy in loads(i):
            copy.wait()

        @pl.loop(i * per_piece, (i + 1) * per_piece)
        def _(block):
            max_slots[me, pl.ds(block, 1), :] = jnp.max(jnp.abs(delta(block)).T, axis=0, keepdims=True)

    momentum_copy.start()
    pl.semaphore_wait(barrier, workers + shards - 2)

    def max_copy(step):
        return pltpu.make_async_remote_copy(
            src_ref=max_slots.at[me], dst_ref=max_slots.at[me],
            send_sem=max_send.at[step], recv_sem=max_recv.at[step],
            device_id={"replica": peer(step)}, device_id_type=MESH,
        )

    @pl.loop(1, workers)
    def _(step):
        max_copy(step).start()

    @pl.loop(1, workers)
    def _(step):
        max_copy(step).wait()

    absmax = max_slots[0]
    for w in range(1, workers):
        absmax = jnp.maximum(absmax, max_slots[w])
    max_out[...] = absmax
    inverse[...] = grid_levels / (absmax + epsilon)
    spread[...] = (absmax + epsilon) / (grid_levels * workers)

    def encode(target, rows_at, put):
        for i in range(blocks_each):
            block = target * blocks_each + i
            values = delta(block, rows_at) * column_of(inverse[pl.ds(block, 1), :])[rows_at]
            nearest = (values + SHIFT) - SHIFT
            rest = smooth_rest(smooth_rest(values - nearest))
            put(i, (nearest + rest).astype(jnp.bfloat16))

    def far_first(turn):
        return 1 + lax.rem(turn - 1 + (workers // 2 - 1), workers - 1)

    def enc_copy(part, turn):
        step = far_first(turn)
        return pltpu.make_async_remote_copy(
            src_ref=encoded.at[part, peer(step)], dst_ref=arrived.at[part, me],
            send_sem=enc_send.at[part, step], recv_sem=enc_recv.at[part, step],
            device_id={"replica": peer(step)}, device_id_type=MESH,
        )

    for part in range(parts):
        rows_at = slice(part * half, (part + 1) * half)

        @pl.loop(1, workers)
        def _(turn):
            target = peer(far_first(turn))

            def put(i, value):
                encoded[part, target, :, i * BLOCK : (i + 1) * BLOCK] = value

            encode(target, rows_at, put)

            @pl.when(turn > 1)
            def _():
                enc_copy(part, turn - 1).start()

        def put_own(i, value):
            total[rows_at, i * BLOCK : (i + 1) * BLOCK] = value.astype(jnp.float32)

        encode(me, rows_at, put_own)
        enc_copy(part, workers - 1).start()

    pairs = workers // 2
    low = lax.rem(me, 2)
    high = me // 2
    partner = me + 1 - 2 * low

    def place(worker, part):
        return grad_out.at[
            part * half : (part + 1) * half, pl.ds(pl.multiple_of(worker * width, BLOCK), width)
        ]

    def ring_origin(step):
        return lax.rem(high + pairs - step, pairs) * 2 + low

    def gat_copy(part, step):
        return pltpu.make_async_remote_copy(
            src_ref=share.at[part], dst_ref=place(me, part),
            send_sem=gat_send.at[part, step], recv_sem=gat_recv.at[part, step],
            device_id={"replica": lax.rem(high + step, pairs) * 2 + low}, device_id_type=MESH,
        )

    def own_forward(part):
        return pltpu.make_async_remote_copy(
            src_ref=share.at[part], dst_ref=place(me, part),
            send_sem=fwd_send.at[part, 0], recv_sem=fwd_recv.at[part, 0],
            device_id={"replica": partner}, device_id_type=MESH,
        )

    def forward(part, step):
        return pltpu.make_async_remote_copy(
            src_ref=place(ring_origin(step), part), dst_ref=place(ring_origin(step), part),
            send_sem=fwd_send.at[part, step], recv_sem=fwd_recv.at[part, step],
            device_id={"replica": partner}, device_id_type=MESH,
        )

    def own_copy(part):
        return pltpu.make_async_copy(share.at[part], place(me, part), own_sem.at[part])

    def sq_copy(step):
        return pltpu.make_async_remote_copy(
            src_ref=squares.at[me], dst_ref=squares.at[me],
            send_sem=sq_send.at[step], recv_sem=sq_recv.at[step],
            device_id={"replica": peer(step)}, device_id_type=MESH,
        )

    square = jnp.zeros((8, BLOCK), jnp.float32)
    for part in range(parts):
        rows_at = slice(part * half, (part + 1) * half)

        @pl.loop(1, workers)
        def _(turn):
            enc_copy(part, turn).wait()
            total[rows_at, :] += arrived[part, origin(far_first(turn))].astype(jnp.float32)

        for i in range(blocks_each):
            block = me * blocks_each + i
            at = slice(i * BLOCK, (i + 1) * BLOCK)
            value = total[rows_at, at] * column_of(spread[pl.ds(block, 1), :])[rows_at]
            share[part, :, at] = value.astype(jnp.bfloat16)
            square = square + jnp.sum((value * value).reshape(half // 8, 8, BLOCK), axis=0)

        if part == parts - 1:
            squares[me] = jnp.broadcast_to(jnp.sum(square, axis=0, keepdims=True), (8, BLOCK))

            @pl.loop(1, workers)
            def _(step):
                sq_copy(step).start()

        own_forward(part).start()

        @pl.loop(1, pairs)
        def _(step):
            gat_copy(part, step).start()

        own_copy(part).start()

    for part in range(parts):

        @pl.loop(1, pairs)
        def _(step):
            gat_copy(part, step).wait_recv()
            forward(part, step).start()

    @pl.loop(1, workers)
    def _(step):
        sq_copy(step).wait()

    part_sum = squares[0]
    for w in range(1, workers):
        part_sum = part_sum + squares[w]
    shard_squares[my_shard] = part_sum

    def ss_copy(step):
        return pltpu.make_async_remote_copy(
            src_ref=shard_squares.at[my_shard], dst_ref=shard_squares.at[my_shard],
            send_sem=ss_send.at[step], recv_sem=ss_recv.at[step],
            device_id={"shard": lax.rem(my_shard + step, shards)}, device_id_type=MESH,
        )

    @pl.loop(1, shards)
    def _(step):
        ss_copy(step).start()

    @pl.loop(1, shards)
    def _(step):
        ss_copy(step).wait()

    part_sum = shard_squares[0]
    for s in range(1, shards):
        part_sum = part_sum + shard_squares[s]
    mean = jnp.sum(part_sum, axis=1, keepdims=True) / entry_count
    root_mean = jnp.sqrt(mean + epsilon)
    factor_out[...] = jnp.broadcast_to(jnp.minimum(1.0, clip_level / root_mean), factor_out.shape)

    for part in range(parts):
        own_copy(part).wait()

        @pl.loop(1, pairs)
        def _(step):
            gat_copy(part, step).wait_send()
            forward(part, step).wait()

        own_forward(part).wait()

    momentum_copy.wait()


def exchange(outer_params, local_params, momentum):
    workers = lax.axis_size("replica")
    shards = lax.axis_size("shard")
    rows, cols = outer_params.shape
    blocks = cols // BLOCK
    width = cols // workers
    parts = 2
    half = rows // parts
    dma = pltpu.SemaphoreType.DMA
    vmem = pl.BlockSpec(memory_space=pltpu.VMEM)
    hbm = pl.BlockSpec(memory_space=pltpu.HBM)
    anywhere = pl.BlockSpec(memory_space=pl.ANY)
    return pl.pallas_call(
        functools.partial(exchange_kernel, workers, shards, rows * shards * cols),
        out_shape=(
            jax.ShapeDtypeStruct((rows, cols), jnp.bfloat16),
            jax.ShapeDtypeStruct((rows, cols), jnp.float32),
            jax.ShapeDtypeStruct((blocks, rows), jnp.float32),
            jax.ShapeDtypeStruct((8, BLOCK), jnp.float32),
        ),
        in_specs=[hbm, hbm, hbm],
        out_specs=(anywhere, anywhere, vmem, vmem),
        scratch_shapes=[
            pltpu.VMEM((rows, cols), jnp.float32),
            pltpu.VMEM((rows, cols), jnp.bfloat16),
            pltpu.VMEM((workers, blocks, rows), jnp.float32),
            pltpu.VMEM((blocks, rows), jnp.float32),
            pltpu.VMEM((blocks, rows), jnp.float32),
            pltpu.VMEM((parts, workers, half, width), jnp.bfloat16),
            pltpu.VMEM((parts, workers, half, width), jnp.bfloat16),
            pltpu.VMEM((rows, width), jnp.float32),
            pltpu.VMEM((parts, half, width), jnp.bfloat16),
            pltpu.VMEM((workers, 8, BLOCK), jnp.float32),
            pltpu.VMEM((shards, 8, BLOCK), jnp.float32),
            dma((2, 4)),
            dma((workers,)), dma((workers,)),
            dma((parts, workers)), dma((parts, workers)),
            dma((workers,)), dma((workers,)),
            dma((shards,)), dma((shards,)),
            dma((parts, workers // 2)), dma((parts, workers // 2)),
            dma((parts, workers // 2)), dma((parts, workers // 2)),
            dma((parts,)), dma(()),
        ],
        compiler_params=pltpu.CompilerParams(
            collective_id=0, has_side_effects=True, vmem_limit_bytes=16 * 2**20
        ),
        cost_estimate=pl.CostEstimate(
            flops=50 * rows * cols, bytes_accessed=8 * rows * cols * 4, transcendentals=0
        ),
    )(*(pltpu.with_memory_space_constraint(x, pltpu.HBM) for x in (outer_params, local_params, momentum)))


def per_device(outer_params, local_params, momentum):
    gradient, momentum, absmax, factor = exchange(outer_params, local_params, momentum)
    clipped = factor[0, 0] * gradient.astype(jnp.float32)
    momentum_next = outer_decay * momentum + clipped
    params_next = outer_params - outer_rate * (clipped + outer_decay * momentum_next)
    return (params_next, momentum_next, absmax)


def solution(mesh):
    return jax.shard_map(
        per_device,
        mesh=mesh,
        in_specs=(P("shard", None), P("replica", "shard", None), P("shard", None)),
        out_specs=(P("shard", None), P("shard", None), P(None, "shard")),
        check_vma=False,
    )
```

time: 72 us -> 59 us (0.82)
  the two profiles are of different devices: /device:TPU:29 before, /device:TPU:0 now
where the time goes in v2:
time: 59 us; the launch traced here: 58.8 us
  Pallas kernels  53.8 us (91%)
  other arithmetic  3.28 us (6%)
  local copies, waits for them, and re-layouts  1.12 us (2%)
  between operations  0.65 us (1%)
    pallas_call x1, Pallas kernels, exchange(): pl.pallas_call(functools.partial(exchange_kernel, workers, shards, rows *...  53.8 us
    sub x1, other arithmetic, per_device(): outer_params - outer_rate * (clipped + outer_decay * momentum_next)  3.28 us

profile of v2, /device:TPU:0, one launch (start us, length us, event | category | flops | bytes accessed | tf_op | source)
XLA Modules:
  0.0 58.8 jit_solution(9803052475231614474)
XLA Ops:
  0.6 0.0 copy-start
  0.6 53.8 %shard_map.58 = (bf16[128,4096]{1,0:T(8,128)(2,1)S(1)}, f32[128,4096]{1,0:T(8,128)S(1)}, f32[32,128]{1,0:T(8,128)S(1)}, f32[8,128]{1,0:T(8,128)S(1)}) custom-call(f32[128,4096]{1,0:T(8,128)} %outer_hbm.1, bf16[1,128,4096]{2,1,0:T(8,128)(2,1)} %local_hbm.1, f32[128,4096]{1,0:T(8,128)} %momentum_hbm.1), custom_call_target="tpu_custom_call" | custom-call | flops 26214400 | bytes 16777216 | tf_op jit(solution)/shard_map/pallas_call | solution.py:298
  54.4 0.5 slice.3
  54.9 0.0 copy-done
  54.9 3.3 %multiply_subtract_fusion = (f32[128,4096]{1,0:T(8,128)}, f32[128,4096]{1,0:T(8,128)}) fusion(f32[128,4096]{1,0:T(8,128)S(1)} %copy-done, bf16[128,4096]{1,0:T(8,128)(2,1)S(1)} %get-tuple-element.8, f32[]{:T(128)} %bitcast, f32[128,4096]{1,0:T(8,128)S(1)} %get-tuple-element.9), kind=kLoop, calls=%fused_computation | loop fusion | flops 4194304 | bytes 9437188 | tf_op jit(solution)/shard_map/sub | solution.py:342
  58.2 0.6 %copy.7 = f32[32,128]{1,0:T(8,128)} copy(f32[32,128]{1,0:T(8,128)S(1)} %get-tuple-element.18) | data formatting | bytes 32768
Async XLA Ops:
  0.6 54.3 %copy-start = (f32[128,4096]{1,0:T(8,128)S(1)}, f32[128,4096]{1,0:T(8,128)}, u32[]{:S(2)}) copy-start(f32[128,4096]{1,0:T(8,128)} %outer_hbm.1) | copy-start | bytes 6291460

commit v3 on v2

--- a/solution.py
+++ b/solution.py
@@ -83,31 +83,39 @@
         return outer_v[rows_at, at] - local_v[rows_at, at].astype(jnp.float32)
 
     per_piece = piece // BLOCK
+
+    def max_copy(i, step):
+        mine = max_slots.at[me, pl.ds(i * per_piece, per_piece)]
+        return pltpu.make_async_remote_copy(
+            src_ref=mine, dst_ref=mine,
+            send_sem=max_send.at[i, step], recv_sem=max_recv.at[i, step],
+            device_id={"replica": peer(step)}, device_id_type=MESH,
+        )
+
+    together = 4
     for i in range(pieces):
         for copy in loads(i):
             copy.wait()
 
-        @pl.loop(i * per_piece, (i + 1) * per_piece)
-        def _(block):
-            max_slots[me, pl.ds(block, 1), :] = jnp.max(jnp.abs(delta(block)).T, axis=0, keepdims=True)
+        @pl.loop(0, per_piece // together)
+        def _(group):
+            for j in range(together):
+                block = i * per_piece + group * together + j
+                max_slots[me, pl.ds(block, 1), :] = jnp.max(jnp.abs(delta(block)).T, axis=0, keepdims=True)
+
+        if i == 0:
+            pl.semaphore_wait(barrier, workers + shards - 2)
+
+        @pl.loop(1, workers)
+        def _(step):
+            max_copy(i, step).start()
 
     momentum_copy.start()
-    pl.semaphore_wait(barrier, workers + shards - 2)
-
-    def max_copy(step):
-        return pltpu.make_async_remote_copy(
-            src_ref=max_slots.at[me], dst_ref=max_slots.at[me],
-            send_sem=max_send.at[step], recv_sem=max_recv.at[step],
-            device_id={"replica": peer(step)}, device_id_type=MESH,
-        )
-
-    @pl.loop(1, workers)
-    def _(step):
-        max_copy(step).start()
-
-    @pl.loop(1, workers)
-    def _(step):
-        max_copy(step).wait()
+    for i in range(pieces):
+
+        @pl.loop(1, workers)
+        def _(step):
+            max_copy(i, step).wait()
 
     absmax = max_slots[0]
     for w in range(1, workers):
@@ -119,7 +127,7 @@
     def encode(target, rows_at, put):
         for i in range(blocks_each):
             block = target * blocks_each + i
-            values = delta(block, rows_at) * column_of(inverse[pl.ds(block, 1), :])[rows_at]
+            values = delta(block, rows_at) * column_of(inverse[pl.ds(block, 1), :][:, rows_at])
             nearest = (values + SHIFT) - SHIFT
             rest = smooth_rest(smooth_rest(values - nearest))
             put(i, (nearest + rest).astype(jnp.bfloat16))
@@ -213,7 +221,7 @@
         for i in range(blocks_each):
             block = me * blocks_each + i
             at = slice(i * BLOCK, (i + 1) * BLOCK)
-            value = total[rows_at, at] * column_of(spread[pl.ds(block, 1), :])[rows_at]
+            value = total[rows_at, at] * column_of(spread[pl.ds(block, 1), :][:, rows_at])
             share[part, :, at] = value.astype(jnp.bfloat16)
             square = square + jnp.sum((value * value).reshape(half // 8, 8, BLOCK), axis=0)
 
@@ -318,7 +326,7 @@
             pltpu.VMEM((workers, 8, BLOCK), jnp.float32),
             pltpu.VMEM((shards, 8, BLOCK), jnp.float32),
             dma((2, 4)),
-            dma((workers,)), dma((workers,)),
+            dma((4, workers)), dma((4, workers)),
             dma((parts, workers)), dma((parts, workers)),
             dma((workers,)), dma((workers,)),
             dma((shards,)), dma((shards,)),

time: 59 us -> 57.5 us (0.975)
  Pallas kernels: 53.8 us -> 52.3 us
    pallas_call x1, Pallas kernels: 53.8 us -> 52.3 us  [exchange(): pl.pallas_call(functools.partial(exchange_kernel, workers, shards, rows *...]
where the time goes in v3:
time: 57.5 us; the launch traced here: 57.4 us
  Pallas kernels  52.3 us (91%)
  other arithmetic  3.28 us (6%)
  local copies, waits for them, and re-layouts  1.12 us (2%)
  between operations  0.65 us (1%)
    pallas_call x1, Pallas kernels, exchange(): pl.pallas_call(functools.partial(exchange_kernel, workers, shards, rows *...  52.3 us
    sub x1, other arithmetic, per_device(): outer_params - outer_rate * (clipped + outer_decay * momentum_next)  3.28 us

profile of v3, /device:TPU:0, one launch (start us, length us, event | category | flops | bytes accessed | tf_op | source)
XLA Modules:
  0.0 57.4 jit_solution(8752291102367186103)
XLA Ops:
  0.6 0.0 copy-start
  0.6 52.3 %shard_map.58 = (bf16[128,4096]{1,0:T(8,128)(2,1)S(1)}, f32[128,4096]{1,0:T(8,128)S(1)}, f32[32,128]{1,0:T(8,128)S(1)}, f32[8,128]{1,0:T(8,128)S(1)}) custom-call(f32[128,4096]{1,0:T(8,128)} %outer_hbm.1, bf16[1,128,4096]{2,1,0:T(8,128)(2,1)} %local_hbm.1, f32[128,4096]{1,0:T(8,128)} %momentum_hbm.1), custom_call_target="tpu_custom_call" | custom-call | flops 26214400 | bytes 16777216 | tf_op jit(solution)/shard_map/pallas_call | solution.py:306
  53.0 0.5 slice.3
  53.5 0.0 copy-done
  53.5 3.3 %multiply_subtract_fusion = (f32[128,4096]{1,0:T(8,128)}, f32[128,4096]{1,0:T(8,128)}) fusion(f32[128,4096]{1,0:T(8,128)S(1)} %copy-done, bf16[128,4096]{1,0:T(8,128)(2,1)S(1)} %get-tuple-element.8, f32[]{:T(128)} %bitcast, f32[128,4096]{1,0:T(8,128)S(1)} %get-tuple-element.9), kind=kLoop, calls=%fused_computation | loop fusion | flops 4194304 | bytes 9437188 | tf_op jit(solution)/shard_map/sub | solution.py:350
  56.8 0.6 %copy.7 = f32[32,128]{1,0:T(8,128)} copy(f32[32,128]{1,0:T(8,128)S(1)} %get-tuple-element.18) | data formatting | bytes 32768
Async XLA Ops:
  0.6 52.9 %copy-start = (f32[128,4096]{1,0:T(8,128)S(1)}, f32[128,4096]{1,0:T(8,128)}, u32[]{:S(2)}) copy-start(f32[128,4096]{1,0:T(8,128)} %outer_hbm.1) | copy-start | bytes 6291460

commit v4 on v3

--- a/solution.py
+++ b/solution.py
@@ -343,12 +343,72 @@
     )(*(pltpu.with_memory_space_constraint(x, pltpu.HBM) for x in (outer_params, local_params, momentum)))
 
 
+def finish_kernel(
+    factor_ref, outer_ref, gradient_ref, momentum_ref, max_ref, params_out, next_out, max_out,
+    params_v, next_v, sem, max_sem,
+):
+    tiles = sem.shape[1]
+    rows = outer_ref.shape[0] // tiles
+    maxima = pltpu.make_async_copy(max_ref, max_out, max_sem)
+    maxima.start()
+
+    def stores(tile):
+        at = pl.ds(tile * rows, rows)
+        return (
+            pltpu.make_async_copy(next_v.at[at], next_out.at[at], sem.at[0, tile]),
+            pltpu.make_async_copy(params_v.at[at], params_out.at[at], sem.at[1, tile]),
+        )
+
+    factor = factor_ref[0:1, 0:1]
+
+    @pl.loop(0, tiles)
+    def _(tile):
+        at = pl.ds(pl.multiple_of(tile * rows, rows), rows)
+        clipped = factor * gradient_ref[at, :].astype(jnp.float32)
+        momentum_next = outer_decay * momentum_ref[at, :] + clipped
+        next_v[at, :] = momentum_next
+        params_v[at, :] = outer_ref[at, :] - outer_rate * (clipped + outer_decay * momentum_next)
+        for copy in stores(tile):
+            copy.start()
+
+    @pl.loop(0, tiles)
+    def _(tile):
+        for copy in stores(tile):
+            copy.wait()
+
+    maxima.wait()
+
+
+def finish(factor, outer_params, gradient, momentum, absmax):
+    rows, cols = outer_params.shape
+    tiles = rows // 16
+    vmem = pl.BlockSpec(memory_space=pltpu.VMEM)
+    hbm = pl.BlockSpec(memory_space=pltpu.HBM)
+    return pl.pallas_call(
+        finish_kernel,
+        out_shape=(
+            pltpu.HBM((rows, cols), jnp.float32),
+            pltpu.HBM((rows, cols), jnp.float32),
+            pltpu.HBM(absmax.shape, jnp.float32),
+        ),
+        in_specs=[vmem] * 5,
+        out_specs=(hbm, hbm, hbm),
+        scratch_shapes=[
+            pltpu.VMEM((rows, cols), jnp.float32),
+            pltpu.VMEM((rows, cols), jnp.float32),
+            pltpu.SemaphoreType.DMA((2, tiles)),
+            pltpu.SemaphoreType.DMA(()),
+        ],
+        compiler_params=pltpu.CompilerParams(vmem_limit_bytes=16 * 2**20),
+        cost_estimate=pl.CostEstimate(
+            flops=6 * rows * cols, bytes_accessed=18 * rows * cols, transcendentals=0
+        ),
+    )(factor, outer_params, gradient, momentum, absmax)
+
+
 def per_device(outer_params, local_params, momentum):
     gradient, momentum, absmax, factor = exchange(outer_params, local_params, momentum)
-    clipped = factor[0, 0] * gradient.astype(jnp.float32)
-    momentum_next = outer_decay * momentum + clipped
-    params_next = outer_params - outer_rate * (clipped + outer_decay * momentum_next)
-    return (params_next, momentum_next, absmax)
+    return finish(factor, outer_params, gradient, momentum, absmax)
 
 
 def solution(mesh):

time: 57.5 us -> 55.4 us (0.963)
  other arithmetic: 3.28 us -> 0 us
  Pallas kernels: 52.3 us -> 54.6 us
  local copies, waits for them, and re-layouts: 1.12 us -> 0.01 us
    sub x1 -> x0, other arithmetic: 3.28 us -> none  [per_device(): outer_params - outer_rate * (clipped + outer_decay * momentum_next)]
    pallas_call x0 -> x1, Pallas kernels: none -> 2.23 us  [finish(): pl.pallas_call(finish_kernel, out_shape=(pltpu.HBM((rows, cols), jnp.floa...]
    unnamed x3 -> x2, local copies, waits for them, and re-layouts: 0.61 us -> 0.01 us
where the time goes in v4:
time: 55.4 us; the launch traced here: 55.2 us
  Pallas kernels  54.6 us (99%)
  between operations  0.65 us (1%)
    pallas_call x1, Pallas kernels, exchange(): pl.pallas_call(functools.partial(exchange_kernel, workers, shards, rows *...  52.3 us
    pallas_call x1, Pallas kernels, finish(): pl.pallas_call(finish_kernel, out_shape=(pltpu.HBM((rows, cols), jnp.floa...  2.23 us

profile of v4, /device:TPU:0, one launch (start us, length us, event | category | flops | bytes accessed | tf_op | source)
XLA Modules:
  0.0 55.2 jit_solution(493545278055812867)
XLA Ops:
  0.6 0.0 copy-start
  0.6 52.3 %shard_map.58 = (bf16[128,4096]{1,0:T(8,128)(2,1)S(1)}, f32[128,4096]{1,0:T(8,128)S(1)}, f32[32,128]{1,0:T(8,128)S(1)}, f32[8,128]{1,0:T(8,128)S(1)}) custom-call(f32[128,4096]{1,0:T(8,128)} %outer_ref.1, bf16[1,128,4096]{2,1,0:T(8,128)(2,1)} %local_hbm.1, f32[128,4096]{1,0:T(8,128)} %momentum_hbm.1), custom_call_target="tpu_custom_call" | custom-call | flops 26214400 | bytes 16777216 | tf_op jit(solution)/shard_map/pallas_call | solution.py:306
  53.0 0.0 copy-done
  53.0 2.2 %shard_map.59 = (f32[128,4096]{1,0:T(8,128)}, f32[128,4096]{1,0:T(8,128)}, f32[32,128]{1,0:T(8,128)}) custom-call(f32[8,128]{1,0:T(8,128)S(1)} %get-tuple-element.7.factor_ref, f32[128,4096]{1,0:T(8,128)S(1)} %copy-done, bf16[128,4096]{1,0:T(8,128)(2,1)S(1)} %get-tuple-element.8.gradient_ref, f32[128,4096]{1,0:T(8,128)S(1)} %get-tuple-element.9.momentum_ref, ...), custom_call_target="tpu_custom_call" | custom-call | flops 3145728 | bytes 9437184 | tf_op jit(solution)/shard_map/pallas_call | solution.py:387
Async XLA Ops:
  0.6 52.3 %copy-start = (f32[128,4096]{1,0:T(8,128)S(1)}, f32[128,4096]{1,0:T(8,128)}, u32[]{:S(2)}) copy-start(f32[128,4096]{1,0:T(8,128)} %outer_ref.1) | copy-start | bytes 6291460

commit v5 on v4

--- a/solution.py
+++ b/solution.py
@@ -36,7 +36,7 @@
     workers, shards, entry_count,
     outer_hbm, local_hbm, momentum_hbm, grad_out, momentum_out, max_out, factor_out,
     outer_v, local_v, max_slots, inverse, spread, encoded, arrived, total, share, squares, shard_squares,
-    load_sem, max_send, max_recv, enc_send, enc_recv, sq_send, sq_recv, ss_send, ss_recv, gat_send, gat_recv, fwd_send, fwd_recv, own_sem, momentum_sem,
+    load_sem, max_send, max_recv, enc_send, enc_recv, sq_send, sq_recv, ss_send, ss_recv, gat_send, gat_recv, cross_send, cross_recv, relay_send, fwd_send, fwd_recv, own_sem, momentum_sem,
 ):
     me = lax.axis_index("replica")
     my_shard = lax.axis_index("shard")
@@ -175,29 +175,70 @@
             part * half : (part + 1) * half, pl.ds(pl.multiple_of(worker * width, BLOCK), width)
         ]
 
-    def ring_origin(step):
-        return lax.rem(high + pairs - step, pairs) * 2 + low
-
-    def gat_copy(part, step):
+    span = pairs // 2
+    upper = high // span
+    base = upper * span
+    spot = high - base
+    is_gateway = spot == (span - 1) * (1 - upper)
+    other_gateway = span - upper
+
+    def near_first(turn):
+        return turn + upper * (span - 1 - 2 * turn)
+
+    def inner_origin(step):
+        return base + lax.rem(spot + span - step, span)
+
+    def cross_origin(j):
+        return (1 - upper) * span + j
+
+    def inner_copy(part, step):
         return pltpu.make_async_remote_copy(
             src_ref=share.at[part], dst_ref=place(me, part),
             send_sem=gat_send.at[part, step], recv_sem=gat_recv.at[part, step],
-            device_id={"replica": lax.rem(high + step, pairs) * 2 + low}, device_id_type=MESH,
+            device_id={"replica": (base + lax.rem(spot + step, span)) * 2 + low}, device_id_type=MESH,
+        )
+
+    def cross_copy(part):
+        return pltpu.make_async_remote_copy(
+            src_ref=share.at[part], dst_ref=place(me, part),
+            send_sem=cross_send.at[part], recv_sem=cross_recv.at[part, spot],
+            device_id={"replica": other_gateway * 2 + low}, device_id_type=MESH,
+        )
+
+    def relay(part, j, step):
+        chunk = place(cross_origin(j) * 2 + low, part)
+        return pltpu.make_async_remote_copy(
+            src_ref=chunk, dst_ref=chunk,
+            send_sem=relay_send.at[part, j, step], recv_sem=cross_recv.at[part, j],
+            device_id={"replica": (base + lax.rem(spot + step, span)) * 2 + low}, device_id_type=MESH,
         )
 
     def own_forward(part):
         return pltpu.make_async_remote_copy(
             src_ref=share.at[part], dst_ref=place(me, part),
-            send_sem=fwd_send.at[part, 0], recv_sem=fwd_recv.at[part, 0],
+            send_sem=fwd_send.at[part, high], recv_sem=fwd_recv.at[part, high],
             device_id={"replica": partner}, device_id_type=MESH,
         )
 
-    def forward(part, step):
-        return pltpu.make_async_remote_copy(
-            src_ref=place(ring_origin(step), part), dst_ref=place(ring_origin(step), part),
-            send_sem=fwd_send.at[part, step], recv_sem=fwd_recv.at[part, step],
+    def forward(part, row):
+        chunk = place(row * 2 + low, part)
+        return pltpu.make_async_remote_copy(
+            src_ref=chunk, dst_ref=chunk,
+            send_sem=fwd_send.at[part, row], recv_sem=fwd_recv.at[part, row],
             device_id={"replica": partner}, device_id_type=MESH,
         )
+
+    def take_cross(part, turn):
+        j = near_first(turn)
+        relay(part, j, 1).wait_recv()
+
+        @pl.when(is_gateway)
+        def _():
+            @pl.loop(1, span)
+            def _(step):
+                relay(part, j, step).start()
+
+        forward(part, cross_origin(j)).start()
 
     def own_copy(part):
         return pltpu.make_async_copy(share.at[part], place(me, part), own_sem.at[part])
@@ -232,20 +273,27 @@
             def _(step):
                 sq_copy(step).start()
 
+        cross_copy(part).start()
         own_forward(part).start()
 
-        @pl.loop(1, pairs)
+        @pl.loop(1, span)
         def _(step):
-            gat_copy(part, step).start()
+            inner_copy(part, step).start()
 
         own_copy(part).start()
 
     for part in range(parts):
 
-        @pl.loop(1, pairs)
+        take_cross(part, 0)
+
+        @pl.loop(1, span)
         def _(step):
-            gat_copy(part, step).wait_recv()
-            forward(part, step).start()
+            inner_copy(part, step).wait_recv()
+            forward(part, inner_origin(step)).start()
+
+        @pl.loop(1, span)
+        def _(turn):
+            take_cross(part, turn)
 
     @pl.loop(1, workers)
     def _(step):
@@ -281,12 +329,23 @@
     for part in range(parts):
         own_copy(part).wait()
 
-        @pl.loop(1, pairs)
+        cross_copy(part).wait_send()
+
+        @pl.loop(1, span)
         def _(step):
-            gat_copy(part, step).wait_send()
-            forward(part, step).wait()
-
-        own_forward(part).wait()
+            inner_copy(part, step).wait_send()
+
+        @pl.when(is_gateway)
+        def _():
+            @pl.loop(0, span)
+            def _(j):
+                @pl.loop(1, span)
+                def _(step):
+                    relay(part, j, step).wait_send()
+
+        @pl.loop(0, pairs)
+        def _(row):
+            forward(part, row).wait()
 
     momentum_copy.wait()
 
@@ -330,7 +389,8 @@
             dma((parts, workers)), dma((parts, workers)),
             dma((workers,)), dma((workers,)),
             dma((shards,)), dma((shards,)),
-            dma((parts, workers // 2)), dma((parts, workers // 2)),
+            dma((parts, workers // 4)), dma((parts, workers // 4)),
+            dma((parts,)), dma((parts, workers // 4)), dma((parts, workers // 4, workers // 4)),
             dma((parts, workers // 2)), dma((parts, workers // 2)),
             dma((parts,)), dma(()),
         ],

time: 55.4 us -> 55.4 us (level)
  no operation moved by 1% of the time
where the time goes in v5:
time: 55.4 us; the launch traced here: 55.3 us
  Pallas kernels  54.6 us (99%)
  between operations  0.65 us (1%)
    pallas_call x1, Pallas kernels, exchange(): pl.pallas_call(functools.partial(exchange_kernel, workers, shards, rows *...  52.4 us
    pallas_call x1, Pallas kernels, finish(): pl.pallas_call(finish_kernel, out_shape=(pltpu.HBM((rows, cols), jnp.floa...  2.23 us

profile of v5, /device:TPU:0, one launch (start us, length us, event | category | flops | bytes accessed | tf_op | source)
XLA Modules:
  0.0 55.3 jit_solution(8712110968350892655)
XLA Ops:
  0.6 0.0 copy-start
  0.6 52.4 %shard_map.58 = (bf16[128,4096]{1,0:T(8,128)(2,1)S(1)}, f32[128,4096]{1,0:T(8,128)S(1)}, f32[32,128]{1,0:T(8,128)S(1)}, f32[8,128]{1,0:T(8,128)S(1)}) custom-call(f32[128,4096]{1,0:T(8,128)} %outer_ref.1, bf16[1,128,4096]{2,1,0:T(8,128)(2,1)} %local_hbm.1, f32[128,4096]{1,0:T(8,128)} %momentum_hbm.1), custom_call_target="tpu_custom_call" | custom-call | flops 26214400 | bytes 16777216 | tf_op jit(solution)/shard_map/pallas_call | solution.py:365
  53.0 0.0 copy-done
  53.0 2.2 %shard_map.59 = (f32[128,4096]{1,0:T(8,128)}, f32[128,4096]{1,0:T(8,128)}, f32[32,128]{1,0:T(8,128)}) custom-call(f32[8,128]{1,0:T(8,128)S(1)} %get-tuple-element.7.factor_ref, f32[128,4096]{1,0:T(8,128)S(1)} %copy-done, bf16[128,4096]{1,0:T(8,128)(2,1)S(1)} %get-tuple-element.8.gradient_ref, f32[128,4096]{1,0:T(8,128)S(1)} %get-tuple-element.9.momentum_ref, ...), custom_call_target="tpu_custom_call" | custom-call | flops 3145728 | bytes 9437184 | tf_op jit(solution)/shard_map/pallas_call | solution.py:447
Async XLA Ops:
  0.6 52.4 %copy-start = (f32[128,4096]{1,0:T(8,128)S(1)}, f32[128,4096]{1,0:T(8,128)}, u32[]{:S(2)}) copy-start(f32[128,4096]{1,0:T(8,128)} %outer_ref.1) | copy-start | bytes 6291460
